TPU v7x, 32 devices: a whole 2x2x4 slice. The times are simulated.
32 devices in a mesh: dp: 32 (over z, y, x, core), tensor: 1.
Axes of the slice: x: 2, y: 2, z: 4, core: 2. Of those that a mesh axis runs over, the one named last changes fastest.
Arguments:
- activations: bfloat16 [384, 8192], P('dp', 'tensor'), may hold values from -400 to 400, as said below
- weight: bfloat16 [8192, 28672], P('dp', 'tensor'), may hold values from -0.0625 to 0.0625
Outputs:
- channel_mean: float32 [8192], P('dp')
- column_errors: float32 [4, 28672], P(None, ('tensor', 'dp'))
- errors: float32 [4], replicated
Inputs may be any that keep to these rules, and one draw needn't show every extreme that they name: activations and weight are finite real values within the ranges stated above.
All inputs are finite; a program needn't handle non-finite values.
Results may differ from a plain program's by a relative error of at most 0.0012.
The roundings to bfloat16 on the way count: a program that leaves them out, or rounds other values in their place, can miss the bound.
Values may be sent and summed in bfloat16 or wider, within the bound.
A program may use at most 128 MiB of HBM per device.

v0:
```python
import math

import jax
import jax.numpy as jnp
from jax import lax
from jax.sharding import PartitionSpec as P

D = 8192
F = 28672
GROUP = 128
GRID = 4


def soft_round(values):
    return values - jnp.sin(2.0 * math.pi * values) / (2.0 * math.pi)


def scale_table(channel_mean):
    ratios = jnp.arange(GRID, dtype=jnp.float32) / GRID
    raw = jnp.exp(ratios[:, None] * jnp.log(channel_mean)[None, :])
    top = jnp.max(raw, axis=1, keepdims=True)
    bottom = jnp.min(raw, axis=1, keepdims=True)
    return raw / jnp.sqrt(top * bottom)


def on_device(activations, weight):
    widened = lax.all_gather(activations, "tensor", axis=1, tiled=True)
    gathered = lax.all_gather(widened, "dp", axis=0, tiled=True)
    columns = lax.all_to_all(weight, "dp", split_axis=1, concat_axis=0, tiled=True)
    width = columns.shape[1]
    token_count = gathered.shape[0]
    channel_mean = jnp.sum(jnp.abs(gathered), axis=0, dtype=jnp.float32) / token_count + 1e-06
    scales = scale_table(channel_mean)
    base_out = jnp.dot(gathered, columns, preferred_element_type=jnp.float32)
    weight_float = columns.astype(jnp.float32)

    def local_error(factor):
        scaled = weight_float * factor[:, None]
        grouped = scaled.reshape(D // GROUP, GROUP, width)
        quant_step = (jnp.max(jnp.abs(grouped), axis=1, keepdims=True) + 1e-06) / 7.0
        levels = soft_round(grouped / quant_step)
        dequant = ((levels * quant_step).reshape(D, width) / factor[:, None]).astype(jnp.bfloat16)
        quant_out = jnp.dot(gathered, dequant, preferred_element_type=jnp.float32)
        residue = quant_out - base_out
        return jnp.sum(residue * residue, axis=0)

    column_sums = lax.map(local_error, scales)
    totals = lax.psum(jnp.sum(column_sums, axis=1), ("dp", "tensor"))
    errors = totals / (token_count * F)
    column_errors = column_sums / token_count
    rows = D // lax.axis_size("dp")
    own_mean = lax.dynamic_slice_in_dim(channel_mean, lax.axis_index("dp") * rows, rows)
    return (own_mean, column_errors, errors)


def solution(mesh):
    placed = (P("dp", "tensor"), P("dp", "tensor"))
    return jax.shard_map(
        on_device,
        mesh=mesh,
        in_specs=placed,
        out_specs=(P("dp"), P(None, ("tensor", "dp")), P()),
        check_vma=False,
    )
```

profile of v0, /device:TPU:10, one launch (start us, length us, event | category | flops | bytes accessed | tf_op | source)
XLA Modules:
  0.0 1007.1 jit_solution(17672235524525206103)
XLA Ops:
  7.2 14.7 %copy.10 = bf16[32,32,8,896]{3,2,0,1:T(8,128)(2,1)} copy(bf16[32,32,8,896]{3,2,1,0:T(8,128)(2,1)} %bitcast.49) | data formatting | bytes 29360128 | tf_op jit(solution)/shard_map/all_to_all | solution.py:29
  21.9 6.1 all-to-all-start
  28.7 192.3 %all-gather.3.cloned.1.call-done = bf16[32,12,8192]{2,1,0:T(8,128)(2,1)} async-done(((bf16[1,12,8192]{2,1,0:T(8,128)(2,1)}), bf16[32,12,8192]{2,1,0:T(8,128)(2,1)}) %all-gather.3.cloned.1.call-update) | async-done | bytes 6291472 | tf_op jit(solution)/shard_map/all_gather | solution.py:28
  221.0 8.8 reshape.50
  235.0 147.9 %all-to-all-done = bf16[256,32,896]{2,0,1:T(8,128)(2,1)} async-done(((bf16[256,32,896]{2,0,1:T(8,128)(2,1)}), bf16[256,32,896]{2,0,1:T(8,128)(2,1)}, u32[]{:S(2)}, u32[]{:S(2)}) %all-to-all-start) | async-done | bytes 14680096 | tf_op jit(solution)/shard_map/all_to_all | solution.py:29
  382.9 12.0 %fusion.10 = f32[384,896]{1,0:T(8,128)} fusion(bf16[384,8192]{1,0:T(8,128)(2,1)} %reshape.50, bf16[8192,896]{1,0:T(8,128)(2,1)} %bitcast.7), kind=kOutput, calls=%fused_computation.25 | convolution fusion | flops 5637144576 | bytes 22347776 | tf_op jit(solution)/shard_map/dot_general | solution.py:34
  394.9 16.6 %bitcast_convert_fusion = f32[8192,896]{1,0:T(8,128)} fusion(bf16[256,32,896]{2,0,1:T(8,128)(2,1)} %all-to-all-done), kind=kLoop, calls=%fused_computation.22 | loop fusion | flops 7340032 | bytes 44040192 | tf_op jit(solution)/shard_map/convert_element_type | solution.py:35
  411.4 541.8 %while.10 = (s32[]{:T(128)}, f32[4,896]{1,0:T(4,128)S(1)}, f32[4,8192]{1,0:T(4,128)S(1)}, f32[8192,896]{1,0:T(8,128)}, bf16[384,8192]{1,0:T(8,128)(2,1)}, /*index=5*/f32[384,896]{1,0:T(8,128)}, s32[]{:T(128)}, s32[]{:T(128)}) while((s32[]{:T(128)}, f32[4,896]{1,0:T(4,128)S(1)}, f32[4,8192]{1,0:T(4,128)S(1)}, f32[8192,896]{1,0:T(8,128)}, ...), condition=%wide.region_6.7_spmd, body=%wide.region_3.6_spmd.sunk | while | flops 5718973440 | bytes 214255232 | solution.py:47
  411.5 12.5 %abs_reduce_fusion.2 = f32[64,896]{1,0:T(8,128)S(1)} fusion(f32[64,128]{1,0:T(8,128)S(1)} %bitcast.50, f32[8192,896]{1,0:T(8,128)} %get-tuple-element.110), kind=kLoop, calls=%fused_computation.4.clone.1 | loop fusion | flops 21962752 | bytes 29622272 | tf_op jit(solution)/shard_map/while/body/eval_jaxpr/reduce_max | solution.py:40
  424.0 5.2 copy-done
  429.2 108.3 %fusion.21 = bf16[8192,896]{1,0:T(8,128)(2,1)S(1)} fusion(f32[8192,896]{1,0:T(8,128)S(1)} %copy-done, f32[64,896]{1,0:T(8,128)S(1)} %add_multiply_fusion.2, f32[8192]{0:T(1024)S(1)} %bitcast.51), kind=kLoop, calls=%fused_computation.3.clone.1 | loop fusion | flops 58720256 | bytes 44302336 | tf_op jit(solution)/shard_map/while/body/eval_jaxpr/convert_element_type | solution.py:42
  537.5 9.3 fusion.22
  546.9 12.5 %abs_reduce_fusion.2 = f32[64,896]{1,0:T(8,128)S(1)} fusion(f32[64,128]{1,0:T(8,128)S(1)} %bitcast.50, f32[8192,896]{1,0:T(8,128)} %get-tuple-element.110), kind=kLoop, calls=%fused_computation.4.clone.1 | loop fusion | flops 21962752 | bytes 29622272 | tf_op jit(solution)/shard_map/while/body/eval_jaxpr/reduce_max | solution.py:40
  559.4 5.2 copy-done
  564.7 108.3 %fusion.21 = bf16[8192,896]{1,0:T(8,128)(2,1)S(1)} fusion(f32[8192,896]{1,0:T(8,128)S(1)} %copy-done, f32[64,896]{1,0:T(8,128)S(1)} %add_multiply_fusion.2, f32[8192]{0:T(1024)S(1)} %bitcast.51), kind=kLoop, calls=%fused_computation.3.clone.1 | loop fusion | flops 58720256 | bytes 44302336 | tf_op jit(solution)/shard_map/while/body/eval_jaxpr/convert_element_type | solution.py:42
  673.0 9.2 fusion.22
  682.4 12.5 %abs_reduce_fusion.2 = f32[64,896]{1,0:T(8,128)S(1)} fusion(f32[64,128]{1,0:T(8,128)S(1)} %bitcast.50, f32[8192,896]{1,0:T(8,128)} %get-tuple-element.110), kind=kLoop, calls=%fused_computation.4.clone.1 | loop fusion | flops 21962752 | bytes 29622272 | tf_op jit(solution)/shard_map/while/body/eval_jaxpr/reduce_max | solution.py:40
  700.1 108.3 %fusion.21 = bf16[8192,896]{1,0:T(8,128)(2,1)S(1)} fusion(f32[8192,896]{1,0:T(8,128)S(1)} %copy-done, f32[64,896]{1,0:T(8,128)S(1)} %add_multiply_fusion.2, f32[8192]{0:T(1024)S(1)} %bitcast.51), kind=kLoop, calls=%fused_computation.3.clone.1 | loop fusion | flops 58720256 | bytes 44302336 | tf_op jit(solution)/shard_map/while/body/eval_jaxpr/convert_element_type | solution.py:42
  808.4 9.3 fusion.22
  817.8 12.5 %abs_reduce_fusion.2 = f32[64,896]{1,0:T(8,128)S(1)} fusion(f32[64,128]{1,0:T(8,128)S(1)} %bitcast.50, f32[8192,896]{1,0:T(8,128)} %get-tuple-element.110), kind=kLoop, calls=%fused_computation.4.clone.1 | loop fusion | flops 21962752 | bytes 29622272 | tf_op jit(solution)/shard_map/while/body/eval_jaxpr/reduce_max | solution.py:40
  830.3 5.2 copy-done
  835.6 108.3 %fusion.21 = bf16[8192,896]{1,0:T(8,128)(2,1)S(1)} fusion(f32[8192,896]{1,0:T(8,128)S(1)} %copy-done, f32[64,896]{1,0:T(8,128)S(1)} %add_multiply_fusion.2, f32[8192]{0:T(1024)S(1)} %bitcast.51), kind=kLoop, calls=%fused_computation.3.clone.1 | loop fusion | flops 58720256 | bytes 44302336 | tf_op jit(solution)/shard_map/while/body/eval_jaxpr/convert_element_type | solution.py:42
  943.9 9.3 fusion.22
  954.0 45.8 %psum.7 = f32[4]{0:T(128)S(1)} all-reduce(f32[4]{0:T(128)S(1)} %get-tuple-element.52), channel_id=1, replica_groups=mesh['dp'=32,'tensor'=1] {'dp','tensor'}, use_global_device_ids=true, to_apply=%region_8.9 | all-reduce | flops 4 | bytes 32 | tf_op jit(solution)/shard_map/psum | solution.py:48
  (33 shorter events, 13.0 us)
Async XLA Ops:
  21.9 361.0 %all-to-all-start = ((bf16[256,32,896]{2,0,1:T(8,128)(2,1)}), bf16[256,32,896]{2,0,1:T(8,128)(2,1)}, u32[]{:S(2)}, u32[]{:S(2)}) async-start(bf16[256,32,896]{2,0,1:T(8,128)(2,1)} %bitcast.48), calls=%async_computation | async-start | bytes 29360128 | tf_op jit(solution)/shard_map/all_to_all | solution.py:29
  27.9 193.0 %all-gather.3.cloned.1.call-start = ((), (), s32[]{:S(2)}) async-start(), calls=%async_computation.1 | async-start | bytes 8650752 | tf_op jit(solution)/shard_map/all_gather | solution.py:28
  411.5 17.8 %copy-start = (f32[8192,896]{1,0:T(8,128)S(1)}, f32[8192,896]{1,0:T(8,128)}, u32[]{:S(2)}) copy-start(f32[8192,896]{1,0:T(8,128)} %get-tuple-element.110) | copy-start | bytes 88080384 | tf_op jit(solution)/shard_map/while
  546.9 17.8 %copy-start = (f32[8192,896]{1,0:T(8,128)S(1)}, f32[8192,896]{1,0:T(8,128)}, u32[]{:S(2)}) copy-start(f32[8192,896]{1,0:T(8,128)} %get-tuple-element.110) | copy-start | bytes 88080384 | tf_op jit(solution)/shard_map/while
  682.4 17.8 %copy-start = (f32[8192,896]{1,0:T(8,128)S(1)}, f32[8192,896]{1,0:T(8,128)}, u32[]{:S(2)}) copy-start(f32[8192,896]{1,0:T(8,128)} %get-tuple-element.110) | copy-start | bytes 88080384 | tf_op jit(solution)/shard_map/while
  817.8 17.8 %copy-start = (f32[8192,896]{1,0:T(8,128)S(1)}, f32[8192,896]{1,0:T(8,128)}, u32[]{:S(2)}) copy-start(f32[8192,896]{1,0:T(8,128)} %get-tuple-element.110) | copy-start | bytes 88080384 | tf_op jit(solution)/shard_map/while
Sparse Core Ops, SparseCore 0:
  31.6 189.3 all-gather.2
where the time goes:
time: 1010 us
  other arithmetic  506 us (50%)
  waiting for transfers between devices  341 us (34%)
  matrix products  49 us (5%)
  blocking collectives  45.8 us (5%)
  local copies, waits for them, and re-layouts  45.5 us (5%)
  between operations  14.1 us (1%)
    convert_element_type x4, other arithmetic, local_error(): ((levels * quant_step).reshape(D, width) / factor[:, None]).astype(jnp.bf...  433 us
    all_gather x1, waiting for transfers between devices, on_device(): gathered = lax.all_gather(widened, 'dp', axis=0, tiled=True)  192 us
    all_to_all x1, waiting for transfers between devices, on_device(): lax.all_to_all(weight, 'dp', split_axis=1, concat_axis=0, tiled=True)  148 us
    reduce_max x4, other arithmetic, local_error(): jnp.max(jnp.abs(grouped), axis=1, keepdims=True) + 1e-06  49.8 us
    psum x1, blocking collectives, on_device(): totals = lax.psum(jnp.sum(column_sums, axis=1), ('dp', 'tensor'))  45.8 us
    dot_general x4, matrix products, local_error(): quant_out = jnp.dot(gathered, dequant, preferred_element_type=jnp.float32)  37 us
    while x8, local copies, waits for them, and re-layouts  21 us
  transfers between devices with their start and end apart: 2, of which 2 were waited for; matrix products, arithmetic and copies ran while one was open for 1% of the time, Pallas kernels for 0%

commit v1 on v0

v1 whole, which is shorter than its diff:
```python
import functools
import math

import jax
import jax.numpy as jnp
from jax import lax
from jax.experimental import pallas as pl
from jax.experimental.pallas import tpu as pltpu
from jax.sharding import PartitionSpec as P

GROUP = 128
GRID = 4
LANES = 128
TILE = 256
SINE = (
    6.283182818832115,
    -41.34142141640176,
    81.59618421926638,
    -76.5801034177733,
    41.205405703161745,
    -12.271277356143528,
)


def sine_of_turns(r):
    square = r * r
    value = SINE[-1] * square + SINE[-2]
    for c in SINE[-3::-1]:
        value = value * square + c
    return value * r


def partial_kernel(steps, a_ref, w_ref, s_ref, out_ref, acc, change):
    step = pl.program_id(0)
    depth, width = w_ref.shape

    @pl.when(step == 0)
    def _():
        acc[...] = jnp.zeros_like(acc)

    def tile(start, size):
        def columns(offset, length):
            if isinstance(start, int):
                return pl.ds(start + offset, length)
            return pl.ds(pl.multiple_of(start + offset, LANES), length)

        for k in range(GRID):
            for g in range(depth // GROUP):
                rows = pl.ds(g * GROUP, GROUP)
                for c in range(0, size, LANES):
                    lanes = min(LANES, size - c)
                    w = w_ref[rows, columns(c, lanes)].astype(jnp.float32)
                    scaled = w * s_ref[k, rows, :lanes]
                    top = jnp.max(jnp.abs(scaled), axis=0, keepdims=True)
                    quant_step = (top + 1e-06) / 7.0
                    v = scaled * (1.0 / quant_step)
                    wave = sine_of_turns(v - jnp.round(v))
                    wave = wave * (quant_step * (0.5 / math.pi))
                    dequant = w - wave * s_ref[GRID + k, rows, :lanes]
                    dequant = dequant.astype(jnp.bfloat16).astype(jnp.float32)
                    change[k, rows, pl.ds(c, lanes)] = (dequant - w).astype(jnp.bfloat16)
            acc[k, :, columns(0, size)] += jnp.dot(
                a_ref[...], change[k, :, pl.ds(0, size)], preferred_element_type=jnp.float32
            )

    whole = width // TILE
    if whole:

        @pl.loop(0, whole)
        def _(i):
            tile(i * TILE, TILE)

    if width % TILE:
        tile(whole * TILE, width % TILE)

    @pl.when(step == steps - 1)
    def _():
        for k in range(GRID):
            out_ref[k] = acc[k].astype(out_ref.dtype)


def partial_residue(tokens, columns, table, depth, kind):
    count, channels = tokens.shape
    width = columns.shape[1]
    steps = channels // depth
    return pl.pallas_call(
        functools.partial(partial_kernel, steps),
        grid=(steps,),
        out_shape=jax.ShapeDtypeStruct((GRID, count, width), kind),
        in_specs=[
            pl.BlockSpec((count, depth), lambda i: (0, i)),
            pl.BlockSpec((depth, width), lambda i: (i, 0)),
            pl.BlockSpec((2 * GRID, depth, LANES), lambda i: (0, i, 0)),
        ],
        out_specs=pl.BlockSpec((GRID, count, width), lambda i: (0, 0, 0)),
        scratch_shapes=[
            pltpu.VMEM((GRID, count, width), jnp.float32),
            pltpu.VMEM((GRID, depth, min(TILE, -(-width // LANES) * LANES)), jnp.bfloat16),
        ],
        compiler_params=pltpu.CompilerParams(
            dimension_semantics=("arbitrary",), vmem_limit_bytes=48 << 20
        ),
        cost_estimate=pl.CostEstimate(
            flops=30 * GRID * channels * width * 16,
            bytes_accessed=4 * channels * width,
            transcendentals=0,
        ),
    )(tokens, columns, table)


def on_device(activations, weight):
    n = lax.axis_size("dp")
    half = n // 2
    me = lax.axis_index("dp")
    side, place = me // half, me % half
    groups = [list(range(half)), list(range(half, n))]
    across = [(i, (i + half) % n) for i in range(n)]

    widened = lax.all_gather(activations, "tensor", axis=1, tiled=True)
    own_tokens, channels = widened.shape
    mine = channels // 2
    token_count = own_tokens * n
    kept = lax.dynamic_slice_in_dim(widened, side * mine, mine, axis=1)
    away = lax.dynamic_slice_in_dim(widened, (1 - side) * mine, mine, axis=1)
    other = lax.ppermute(away, "dp", across)
    first = side == 0
    pair = jnp.concatenate([jnp.where(first, kept, other), jnp.where(first, other, kept)], axis=0)
    tokens = lax.all_gather(pair, "dp", axis=0, tiled=True, axis_index_groups=groups)

    width = weight.shape[1]
    away_weight = lax.dynamic_slice_in_dim(weight, (1 - side) * (width // 2), width // 2, axis=1)
    kept_weight = lax.dynamic_slice_in_dim(weight, side * (width // 2), width // 2, axis=1)
    exchange = functools.partial(
        lax.all_to_all, axis_name="dp", split_axis=1, concat_axis=0, tiled=True, axis_index_groups=groups
    )
    away_columns = exchange(away_weight)
    kept_columns = exchange(kept_weight)

    half_mean = jnp.sum(jnp.abs(tokens.astype(jnp.float32)), axis=0) / token_count + 1e-06
    other_mean = lax.ppermute(half_mean, "dp", across)
    ratios = jnp.arange(GRID, dtype=jnp.float32) / GRID
    raw = jnp.exp(ratios[:, None] * jnp.log(half_mean)[None, :])
    raw_other = jnp.exp(ratios[:, None] * jnp.log(other_mean)[None, :])
    top = jnp.maximum(jnp.max(raw, axis=1, keepdims=True), jnp.max(raw_other, axis=1, keepdims=True))
    bottom = jnp.minimum(jnp.min(raw, axis=1, keepdims=True), jnp.min(raw_other, axis=1, keepdims=True))
    scales = raw / jnp.sqrt(top * bottom)
    table = jnp.concatenate([scales, 1.0 / scales], axis=0)
    table = jnp.broadcast_to(table[:, :, None], (2 * GRID, mine, LANES))

    depth = weight.shape[0]
    away_part = partial_residue(tokens, away_columns, table, depth, jnp.bfloat16)
    arrived = lax.ppermute(away_part, "dp", across)
    own_part = partial_residue(tokens, kept_columns, table, depth, jnp.float32)
    residue = own_part + arrived.astype(jnp.float32)
    column_sums = jnp.sum(residue * residue, axis=1)

    totals = lax.psum(jnp.sum(column_sums, axis=1), ("dp", "tensor"))
    errors = totals / (token_count * width * lax.axis_size("tensor"))
    column_errors = column_sums / token_count
    own_mean = lax.dynamic_slice_in_dim(half_mean, place * depth, depth)
    return (own_mean, column_errors, errors)


def solution(mesh):
    placed = (P("dp", "tensor"), P("dp", "tensor"))
    return jax.shard_map(
        on_device,
        mesh=mesh,
        in_specs=placed,
        out_specs=(P("dp"), P(None, ("tensor", "dp")), P()),
        check_vma=False,
    )
```

time: 1010 us -> 576 us (0.57)
  other arithmetic: 506 us -> 9.37 us
  Pallas kernels: 0 us -> 157 us
  waiting for transfers between devices: 341 us -> 271 us
  matrix products: 49 us -> 0 us
  starting transfers between devices: 6.11 us -> 21.5 us
  local copies, waits for them, and re-layouts: 45.5 us -> 60.1 us
    convert_element_type x5 -> x0, other arithmetic: 450 us -> none  [the longest x4 433 us: local_error(): ((levels * quant_step).reshape(D, width) / factor[:, None]).astype(jnp.bf...]
    all_gather x1, waiting for transfers between devices: 192 us -> 32.1 us  [on_device(): lax.all_gather(pair, 'dp', axis=0, tiled=True, axis_index_groups=groups)]
    pallas_call x0 -> x2, Pallas kernels: none -> 157 us  [partial_residue(): pl.pallas_call(functools.partial(partial_kernel, steps), grid=(steps,), o...]
    ppermute x0 -> x3, waiting for transfers between devices: none -> 140 us  [the longest x1 111 us: on_device(): other = lax.ppermute(away, 'dp', across)]
    reduce_max x4 -> x1, other arithmetic: 49.8 us -> 0.26 us  [on_device(): jnp.max(raw_other, axis=1, keepdims=True)]
    all_to_all x1 -> x2, waiting for transfers between devices: 148 us -> 98.7 us  [the longest x1 98.7 us: on_device(): away_columns = exchange(away_weight)]
    dot_general x5 -> x0, matrix products: 49 us -> none  [the longest x4 37 us: local_error(): quant_out = jnp.dot(gathered, dequant, preferred_element_type=jnp.float32)]
    while x8 -> x0, local copies, waits for them, and re-layouts: 21 us -> none
  transfers between devices with their start and end apart: 2 -> 6, of which waited for: 2 -> 5; matrix products, arithmetic and copies ran while one was open for 1% -> 8% of each run, Pallas kernels for 0% -> 27%
where the time goes in v1:
time: 576 us; the launch traced here: 575 us
  waiting for transfers between devices  271 us (47%)
  Pallas kernels  157 us (27%)
  local copies, waits for them, and re-layouts  60.1 us (10%)
  blocking collectives  41.3 us (7%)
  starting transfers between devices  21.5 us (4%)
  between operations  14.1 us (2%)
  other arithmetic  9.37 us (2%)
    pallas_call x2, Pallas kernels, partial_residue(): pl.pallas_call(functools.partial(partial_kernel, steps), grid=(steps,), o...  157 us
    ppermute x1, waiting for transfers between devices, on_device(): other = lax.ppermute(away, 'dp', across)  111 us
    all_to_all x1, waiting for transfers between devices, on_device(): away_columns = exchange(away_weight)  98.7 us
    psum x1, blocking collectives, on_device(): totals = lax.psum(jnp.sum(column_sums, axis=1), ('dp', 'tensor'))  41.3 us
    all_gather x1, waiting for transfers between devices, on_device(): lax.all_gather(pair, 'dp', axis=0, tiled=True, axis_index_groups=groups)  32.1 us
    ppermute x1, waiting for transfers between devices, on_device(): arrived = lax.ppermute(away_part, 'dp', across)  26.5 us
    unnamed x6, local copies, waits for them, and re-layouts  20.1 us
  transfers between devices with their start and end apart: 6, of which 5 were waited for; matrix products, arithmetic and copies ran while one was open for 8% of the time, Pallas kernels for 27%

profile of v1, /device:TPU:10, one launch (start us, length us, event | category | flops | bytes accessed | tf_op | source)
XLA Modules:
  0.0 574.6 jit_solution(3733999944464989298)
XLA Ops:
  7.2 10.6 %constant_dynamic-slice_fusion = (bf16[256,14336]{1,0:T(8,128)(2,1)}, bf16[256,14336]{1,0:T(8,128)(2,1)}) fusion(bf16[256,28672]{1,0:T(8,128)(2,1)} %param.3, s32[]{:T(128)S(6)} %select_n.47, s32[]{:T(128)S(6)} %select_n.46), kind=kLoop, calls=%fused_computation.18 | loop fusion | bytes 29360136 | tf_op jit(solution)/shard_map/dynamic_slice | solution.py:131
  17.8 10.0 %copy.10 = bf16[256,14336]{0,1:T(8,128)(2,1)} copy(bf16[256,14336]{1,0:T(8,128)(2,1)} %get-tuple-element.11) | data formatting | bytes 14680064
  27.8 5.2 all-to-all-start.1
  33.0 10.1 %copy.9 = bf16[256,14336]{0,1:T(8,128)(2,1)} copy(bf16[256,14336]{1,0:T(8,128)(2,1)} %get-tuple-element.12) | data formatting | bytes 14680064
  43.1 98.7 %all-to-all-done.1 = bf16[256,16,896]{0,2,1:T(8,128)(2,1)} async-done(((bf16[256,16,896]{0,2,1:T(8,128)(2,1)}), bf16[256,16,896]{0,2,1:T(8,128)(2,1)}, u32[]{:S(2)}, u32[]{:S(2)}) %all-to-all-start.1) | async-done | bytes 7340064 | tf_op jit(solution)/shard_map/all_to_all | solution.py:136
  141.8 8.8 %all-to-all-start = ((bf16[256,16,896]{0,2,1:T(8,128)(2,1)}), bf16[256,16,896]{0,2,1:T(8,128)(2,1)}, u32[]{:S(2)}, u32[]{:S(2)}) async-start(bf16[256,16,896]{0,2,1:T(8,128)(2,1)} %bitcast.7), calls=%async_computation | async-start | bytes 14680064 | tf_op jit(solution)/shard_map/all_to_all | solution.py:137
  150.7 2.7 collective-permute-start
  153.4 111.3 %collective-permute-done = bf16[12,4096]{1,0:T(8,128)(2,1)S(1)} collective-permute-done((bf16[12,4096]{1,0:T(8,128)(2,1)S(1)}, bf16[12,4096]{1,0:T(8,128)(2,1)S(1)}, u32[]{:S(2)}, u32[]{:S(2)}) %collective-permute-start) | collective-permute-done | bytes 98336 | tf_op jit(solution)/shard_map/ppermute | solution.py:125
  264.7 0.7 pad_maximum_fusion
  265.5 32.1 %all-gather.2.cloned.1.call-done.a_ref = bf16[384,4096]{1,0:T(8,128)(2,1)} async-done(((bf16[24,4096]{1,0:T(8,128)(2,1)}), bf16[384,4096]{1,0:T(8,128)(2,1)}) %all-gather.2.cloned.1.call-update) | async-done | bytes 3145744 | tf_op jit(solution)/shard_map/all_gather | solution.py:128
  297.5 2.6 abs_reduce_fusion
  300.1 2.5 collective-permute-start.1
  302.6 2.2 collective-permute-done.1
  305.3 11.2 %copy.8 = bf16[16,256,896]{2,1,0:T(8,128)(2,1)} copy(bf16[16,256,896]{1,2,0:T(8,128)(2,1)} %bitcast.4) | data formatting | bytes 14680064 | tf_op jit(solution)/shard_map/all_to_all | solution.py:136
  316.5 6.2 %broadcast_in_dim.2.s_ref = f32[8,4096,128]{2,1,0:T(8,128)} broadcast(f32[8,4096]{1,0:T(8,128)S(1)} %pad_maximum_fusion.1), dimensions={0,1} | broadcast | bytes 16908288 | tf_op jit(solution)/shard_map/broadcast_in_dim | solution.py:148
  322.7 78.2 %shard_map.50 = bf16[4,384,896]{2,1,0:T(8,128)(2,1)} custom-call(bf16[384,4096]{1,0:T(8,128)(2,1)S(1)} %copy-done, bf16[4096,896]{1,0:T(8,128)(2,1)} %bitcast.6, f32[8,4096,128]{2,1,0:T(8,128)} %broadcast_in_dim.2.s_ref), custom_call_target="tpu_custom_call" | custom-call | flops 7046430720 | bytes 14680064 | tf_op jit(solution)/shard_map/pallas_call | solution.py:86
  400.9 2.4 collective-permute-start.2
  403.3 0.6 dynamic_slice.17
  404.0 11.2 %copy.6 = bf16[16,256,896]{2,1,0:T(8,128)(2,1)} copy(bf16[16,256,896]{1,2,0:T(8,128)(2,1)} %bitcast.1) | data formatting | bytes 14680064 | tf_op jit(solution)/shard_map/all_to_all | solution.py:137
  415.2 79.1 %shard_map.49 = f32[4,384,896]{2,1,0:T(8,128)} custom-call(bf16[384,4096]{1,0:T(8,128)(2,1)S(1)} %copy-done, bf16[4096,896]{1,0:T(8,128)(2,1)} %bitcast.9, f32[8,4096,128]{2,1,0:T(8,128)} %broadcast_in_dim.2.s_ref), custom_call_target="tpu_custom_call" | custom-call | flops 7046430720 | bytes 14680064 | tf_op jit(solution)/shard_map/pallas_call | solution.py:86
  494.3 26.5 %collective-permute-done.2 = bf16[4,384,896]{2,1,0:T(8,128)(2,1)} collective-permute-done((bf16[4,384,896]{2,1,0:T(8,128)(2,1)}, bf16[4,384,896]{2,1,0:T(8,128)(2,1)}, u32[]{:S(2)}, u32[]{:S(2)}) %collective-permute-start.2) | collective-permute-done | bytes 2752544 | tf_op jit(solution)/shard_map/ppermute | solution.py:152
  520.8 4.4 fusion
  525.3 41.3 %psum.7 = f32[4]{0:T(128)S(1)} all-reduce(f32[4]{0:T(128)S(1)} %get-tuple-element.3), channel_id=1, replica_groups=mesh['dp'=32,'tensor'=1] {'dp','tensor'}, use_global_device_ids=true, to_apply=%region_7.8 | all-reduce | flops 4 | bytes 32 | tf_op jit(solution)/shard_map/psum | solution.py:157
  567.1 0.6 broadcast_multiply_fusion
  (17 shorter events, 1.1 us)
Async XLA Ops:
  27.8 114.0 %all-to-all-start.1 = ((bf16[256,16,896]{0,2,1:T(8,128)(2,1)}), bf16[256,16,896]{0,2,1:T(8,128)(2,1)}, u32[]{:S(2)}, u32[]{:S(2)}) async-start(bf16[256,16,896]{0,2,1:T(8,128)(2,1)} %bitcast.8), calls=%async_computation.1 | async-start | bytes 14680064 | tf_op jit(solution)/shard_map/all_to_all | solution.py:136
  141.8 8.8 %copy-start.1 = (bf16[12,8192]{1,0:T(8,128)(2,1)S(1)}, bf16[12,8192]{1,0:T(8,128)(2,1)}, u32[]{:S(2)}) copy-start(bf16[12,8192]{1,0:T(8,128)(2,1)} %param.2) | copy-start | bytes 589828
  141.8 262.1 %all-to-all-start = ((bf16[256,16,896]{0,2,1:T(8,128)(2,1)}), bf16[256,16,896]{0,2,1:T(8,128)(2,1)}, u32[]{:S(2)}, u32[]{:S(2)}) async-start(bf16[256,16,896]{0,2,1:T(8,128)(2,1)} %bitcast.7), calls=%async_computation | async-start | bytes 14680064 | tf_op jit(solution)/shard_map/all_to_all | solution.py:137
  150.6 146.9 %all-gather.2.cloned.1.call-start = ((), (), s32[]{:S(2)}) async-start(), calls=%async_computation.2 | async-start | bytes 3342336 | tf_op jit(solution)/shard_map/all_gather | solution.py:128
  150.7 114.0 %collective-permute-start = (bf16[12,4096]{1,0:T(8,128)(2,1)S(1)}, bf16[12,4096]{1,0:T(8,128)(2,1)S(1)}, u32[]{:S(2)}, u32[]{:S(2)}) collective-permute-start(bf16[12,4096]{1,0:T(8,128)(2,1)S(1)} %constant_dynamic-slice_fusion.2), channel_id=1, source_target_pairs={{0,16},{1,17},{2,18},{3,19},{4,20},{5,21},{6,22},{7,23},{8,24},{9,... | collective-permute-start | bytes 294920 | tf_op jit(solution)/shard_map/ppermute | solution.py:125
  300.1 4.7 collective-permute-start.1
  316.5 6.2 %copy-start = (bf16[384,4096]{1,0:T(8,128)(2,1)S(1)}, bf16[384,4096]{1,0:T(8,128)(2,1)}, u32[]{:S(2)}) copy-start(bf16[384,4096]{1,0:T(8,128)(2,1)} %all-gather.2.cloned.1.call-done.a_ref) | copy-start | bytes 9437188
  400.9 119.9 %collective-permute-start.2 = (bf16[4,384,896]{2,1,0:T(8,128)(2,1)}, bf16[4,384,896]{2,1,0:T(8,128)(2,1)}, u32[]{:S(2)}, u32[]{:S(2)}) collective-permute-start(bf16[4,384,896]{2,1,0:T(8,128)(2,1)} %shard_map.50), channel_id=1, source_target_pairs={{0,16},{1,17},{2,18},{3,19},{4,20},{5,21},{6,22},{7,23},{8,24},{9,... | collective-permute-start | bytes 8257544 | tf_op jit(solution)/shard_map/ppermute | solution.py:152
Sparse Core Ops, SparseCore 0:
  265.6 31.8 all-gather.1
